TPU v7x, 256 devices: a whole 4x4x8 slice. The times are simulated.
256 devices in a mesh: fft: 32 (over z, x_lo, core), band: 8 (over y, x_hi).
Axes of the slice: x: 4 (x_hi: 2, x_lo: 2; x = x_hi * 2 + x_lo), y: 4, z: 8, core: 2. Of those that a mesh axis runs over, the one named last changes fastest.
Arguments:
- wavefunctions: float32 [2, 16, 128, 128, 128], P(None, 'band', 'fft'), may hold values from -6 to 6
- potential: float32 [128, 128, 128], P('fft'), may hold values from -30 to 10
- occupation: float32 [16], P('band'), may hold values from 0.0125 to 0.25
Outputs:
- propagated: float32 [2, 16, 128, 128, 128], P(None, 'band', 'fft')
- reduced_gradient: float32 [128, 128, 128], P('fft', 'band')
- exchange_density: float32 [128, 128, 128], P('fft', 'band')
All inputs are finite; a program needn't handle non-finite values.
Results may differ from a plain program's by a relative error of at most 0.0003.
Values sent between devices are 32-bit elements; how exact they have to be, the bound alone decides.
A program may use at most 64 MiB of HBM per device.

v0:
```python
import functools
import math

import jax
import jax.numpy as jnp
import numpy as np
from jax import lax
from jax.experimental import pallas as pl
from jax.experimental.pallas import tpu as pltpu
from jax.sharding import PartitionSpec as P

SPACING = 0.4
TIME_STEP = 0.012
HALF_SQUARE = 0.5 * TIME_STEP * TIME_STEP
KAPPA_PBE = 0.804
MU_PBE = 0.21951
FERMI_FACTOR = 2.0 * math.pow(3.0 * math.pi * math.pi, 1.0 / 3.0)
SLATER_FACTOR = 0.75 * math.pow(3.0 / math.pi, 1.0 / 3.0)

GRID = 128
FFT = 32
BAND = 8
PLANES = GRID // FFT
ROWS = 8
OWN_ROWS = GRID // BAND
MESH = pl.DeviceIdType.MESH
F32 = jnp.float32
BF16 = jnp.bfloat16


def kinetic_matrix():
    counter = np.arange(GRID)
    signed = np.where(counter < GRID // 2, counter, counter - GRID)
    half_squares = 0.5 * (2.0 * np.pi * signed / (GRID * SPACING)) ** 2
    phase = np.outer(counter, counter) % GRID
    column = np.cos(2.0 * np.pi * phase / GRID) @ half_squares / GRID
    return column[(counter[:, None] - counter[None, :]) % GRID]


def kinetic_parts():
    matrix = kinetic_matrix()
    high = matrix.astype(jnp.bfloat16)
    low = (matrix - high.astype(np.float64)).astype(jnp.bfloat16)
    return np.stack([high, low])


def split(values):
    high = values.astype(BF16)
    return high, (values - high.astype(F32)).astype(BF16)


def dot(a, b):
    return jnp.dot(a, b, preferred_element_type=F32)


def from_left(table, values):
    high, low = split(values)
    return dot(table[0], high) + dot(table[0], low) + dot(table[1], high)


def in_plane(table, values):
    high, low = split(values)
    left = dot(table[0], high) + dot(table[0], low) + dot(table[1], high)
    right = dot(high, table[0]) + dot(low, table[0]) + dot(high, table[1])
    return left + right


def wait_bytes(ref, sem):
    pltpu.make_async_copy(ref, ref, sem).wait()


def kernel(
    occ,
    psi_hbm,
    pot_hbm,
    table_hbm,
    out_hbm,
    reduced_ref,
    energy_ref,
    psi,
    pot,
    table,
    tang,
    local,
    col,
    col_pot,
    back,
    ret,
    part,
    arrived,
    dens,
    halo_z,
    edge_x,
    halo_x,
    rows_x,
    sem_in,
    sem_out,
    sem_col,
    sem_tang,
    sem_ret,
    sem_group,
    sem_pot,
    sem_dens,
    sem_halo,
    send,
):
    me = lax.axis_index("fft")
    my_band = lax.axis_index("band")
    my_slot = me // 2
    my_chip = me // 4

    def fft_peer(step):
        k = (step + 1) // 2
        sign = 2 * (step % 2) - 1
        return lax.rem(me + sign * k + FFT, FFT)

    def rows_of(slot):
        return pl.ds(pl.multiple_of(slot * ROWS, ROWS), ROWS)

    def planes_of(device):
        return pl.ds(device * PLANES, PLANES)

    barrier = pltpu.get_barrier_semaphore()
    load_psi = pltpu.make_async_copy(psi_hbm, psi, sem_in.at[0])
    load_pot = pltpu.make_async_copy(pot_hbm, pot, sem_in.at[1])
    load_table = pltpu.make_async_copy(table_hbm, table, sem_in.at[2])
    load_psi.start()
    load_pot.start()
    load_table.start()

    @pl.loop(1, FFT)
    def _(step):
        pl.semaphore_signal(
            barrier, inc=1, device_id={"fft": fft_peer(step)}, device_id_type=MESH
        )

    @pl.loop(1, BAND)
    def _(step):
        pl.semaphore_signal(
            barrier,
            inc=1,
            device_id={"band": lax.rem(my_band + step, BAND)},
            device_id_type=MESH,
        )

    load_psi.wait()
    load_pot.wait()
    load_table.wait()
    pl.semaphore_wait(barrier, FFT + BAND - 2)

    @pl.loop(1, FFT)
    def _(step):
        peer = fft_peer(step)
        pltpu.make_async_remote_copy(
            src_ref=psi.at[:, peer % 2, :, rows_of(peer // 2), :],
            dst_ref=col.at[pl.ds(0, 2), planes_of(me)],
            send_sem=send.at[0],
            recv_sem=sem_col,
            device_id={"fft": peer},
            device_id_type=MESH,
        ).start()

    pltpu.make_async_copy(
        psi.at[:, me % 2, :, rows_of(my_slot), :],
        col.at[pl.ds(0, 2), planes_of(me)],
        sem_col,
    ).start()

    first_slot = lax.rem(my_band - me + FFT, BAND)
    for k in range(4):
        target = 2 * (first_slot + BAND * (k // 2)) + k % 2

        @pl.when(target != me)
        def _():
            pltpu.make_async_remote_copy(
                src_ref=pot.at[:, rows_of(target // 2), :],
                dst_ref=col_pot.at[planes_of(me)],
                send_sem=send.at[1],
                recv_sem=sem_pot.at[0],
                device_id={"fft": target},
                device_id_type=MESH,
            ).start()

        @pl.when(target == me)
        def _():
            pltpu.make_async_copy(
                pot.at[:, rows_of(my_slot), :],
                col_pot.at[planes_of(me)],
                sem_pot.at[0],
            ).start()

    kin = (table[0], table[1])

    for part_of in range(2):

        @pl.loop(0, 8)
        def _(index):
            band, plane = index // 4, index % 4
            tang[part_of, band, plane] = in_plane(kin, psi[part_of, band, plane])

        @pl.loop(1, FFT)
        def _(step):
            peer = fft_peer(step)
            pltpu.make_async_remote_copy(
                src_ref=tang.at[part_of, peer % 2, :, rows_of(peer // 2), :],
                dst_ref=col.at[2 + part_of, planes_of(me)],
                send_sem=send.at[2],
                recv_sem=sem_tang.at[part_of],
                device_id={"fft": peer},
                device_id_type=MESH,
            ).start()

        pltpu.make_async_copy(
            tang.at[part_of, me % 2, :, rows_of(my_slot), :],
            col.at[2 + part_of, planes_of(me)],
            sem_tang.at[part_of],
        ).start()

    wait_bytes(col_pot.at[pl.ds(0, 16)], sem_pot.at[0])
    first_device = lax.rem(my_band - my_slot + FFT, BAND)

    @pl.loop(0, 4)
    def _(k):
        held = planes_of(first_device + BAND * k)

        @pl.loop(1, BAND)
        def _(step):
            pltpu.make_async_remote_copy(
                src_ref=col_pot.at[held],
                dst_ref=col_pot.at[held],
                send_sem=send.at[3],
                recv_sem=sem_pot.at[1],
                device_id={"band": lax.rem(my_band + step, BAND)},
                device_id_type=MESH,
            ).start()

    @pl.loop(0, 8)
    def _(index):
        band, plane = index // 4, index % 4
        values = pot[plane]
        real, imag = psi[0, band, plane], psi[1, band, plane]
        first_real = tang[0, band, plane] + values * real
        first_imag = tang[1, band, plane] + values * imag
        second_real = in_plane(kin, first_real) + values * first_real
        second_imag = in_plane(kin, first_imag) + values * first_imag
        local[0, band, plane] = real + TIME_STEP * first_imag - HALF_SQUARE * second_real
        local[1, band, plane] = imag - TIME_STEP * first_real - HALF_SQUARE * second_imag

    wait_bytes(col.at[pl.ds(0, 2)], sem_col)
    wait_bytes(col_pot.at[pl.ds(0, 112)], sem_pot.at[1])
    for part_of in range(2):
        sign = 1.0 - 2.0 * part_of
        wait_bytes(col.at[2 + part_of], sem_tang.at[part_of])

        @pl.loop(0, ROWS)
        def _(row):
            values = col_pot[:, row, :]
            mine = col[part_of, :, row, :]
            other = col[1 - part_of, :, row, :]
            along = from_left(kin, mine)
            inner = (
                (sign * TIME_STEP) * other
                - (2.0 * HALF_SQUARE) * col[2 + part_of, :, row, :]
                - HALF_SQUARE * (values * mine + along)
            )
            back[part_of, :, row, :] = from_left(kin, inner) - HALF_SQUARE * (values * along)

        @pl.loop(1, FFT)
        def _(step):
            peer = fft_peer(step)
            pltpu.make_async_remote_copy(
                src_ref=back.at[part_of, planes_of(peer)],
                dst_ref=ret.at[part_of, me % 2, :, rows_of(my_slot), :],
                send_sem=send.at[4],
                recv_sem=sem_ret if part_of == 0 else sem_group.at[my_chip],
                device_id={"fft": peer},
                device_id_type=MESH,
            ).start()

        pltpu.make_async_copy(
            back.at[part_of, planes_of(me)],
            ret.at[part_of, me % 2, :, rows_of(my_slot), :],
            sem_ret if part_of == 0 else sem_group.at[my_chip],
        ).start()

    wait_bytes(ret.at[0], sem_ret)

    @pl.loop(0, PLANES)
    def _(plane):
        low = local[0, 0, plane] + ret[0, 0, plane]
        high = local[0, 1, plane] + ret[0, 1, plane]
        local[0, 0, plane] = low
        local[0, 1, plane] = high
        part[plane] = occ[0] * (low * low) + occ[1] * (high * high)

    store_real = pltpu.make_async_copy(local.at[0], out_hbm.at[0], sem_out.at[0])
    store_real.start()

    @pl.loop(0, BAND)
    def _(step):
        k = (step + 1) // 2
        sign = 2 * (step % 2) - 1
        block = lax.rem(my_chip + sign * k + BAND, BAND)
        rows = pl.ds(pl.multiple_of(block * OWN_ROWS, OWN_ROWS), OWN_ROWS)
        wait_bytes(ret.at[1, :, :, pl.ds(0, OWN_ROWS), :], sem_group.at[block])
        low = local[1, 0, :, rows, :] + ret[1, 0, :, rows, :]
        high = local[1, 1, :, rows, :] + ret[1, 1, :, rows, :]
        local[1, 0, :, rows, :] = low
        local[1, 1, :, rows, :] = high
        part[:, rows, :] = part[:, rows, :] + (occ[0] * (low * low) + occ[1] * (high * high))

        @pl.when(block != my_band)
        def _():
            pltpu.make_async_remote_copy(
                src_ref=part.at[:, rows, :],
                dst_ref=arrived.at[my_band],
                send_sem=send.at[5],
                recv_sem=sem_dens,
                device_id={"band": block},
                device_id_type=MESH,
            ).start()

        @pl.when(block == my_band)
        def _():
            pltpu.make_async_copy(part.at[:, rows, :], arrived.at[my_band], sem_dens).start()

    store_imag = pltpu.make_async_copy(local.at[1], out_hbm.at[1], sem_out.at[1])
    store_imag.start()

    wait_bytes(arrived, sem_dens)
    total = arrived[0]
    for k in range(1, BAND):
        total = total + arrived[k]
    dens[...] = total
    rows_x[:, 8:24, :] = total
    edge_x[0] = dens[:, 14:16, :]
    edge_x[1] = dens[:, 0:2, :]

    halos = []
    for side in range(2):
        shift = 1 - 2 * side
        halos.append(
            pltpu.make_async_remote_copy(
                src_ref=dens.at[pl.ds(2 - 2 * side, 2)],
                dst_ref=halo_z.at[side],
                send_sem=send.at[6 + side],
                recv_sem=sem_halo.at[side],
                device_id={"fft": lax.rem(me + shift + FFT, FFT)},
                device_id_type=MESH,
            )
        )
        halos.append(
            pltpu.make_async_remote_copy(
                src_ref=edge_x.at[side],
                dst_ref=halo_x.at[side],
                send_sem=send.at[8 + side],
                recv_sem=sem_halo.at[2 + side],
                device_id={"band": lax.rem(my_band + shift + BAND, BAND)},
                device_id_type=MESH,
            )
        )
    for halo in halos:
        halo.start()

    scale = 1.0 / (12.0 * SPACING)
    grad_y = (
        8.0 * (pltpu.roll(total, GRID - 1, 2) - pltpu.roll(total, 1, 2))
        - (pltpu.roll(total, GRID - 2, 2) - pltpu.roll(total, 2, 2))
    ) * scale
    power = jnp.exp((4.0 / 3.0) * jnp.log(total))

    wait_bytes(col.at[pl.ds(0, 2), pl.ds(0, 124)], send.at[0])
    wait_bytes(col.at[pl.ds(0, 2), pl.ds(0, 124)], send.at[2])
    wait_bytes(back.at[:, pl.ds(0, 124)], send.at[4])
    wait_bytes(col_pot.at[pl.ds(0, 112)], send.at[3])
    wait_bytes(arrived.at[pl.ds(0, 7)], send.at[5])
    holds_own = lax.rem(me + my_slot - my_band + FFT, BAND) == 0

    @pl.when(holds_own)
    def _():
        wait_bytes(col_pot.at[pl.ds(0, 12)], send.at[1])

    @pl.when(jnp.logical_not(holds_own))
    def _():
        wait_bytes(col_pot.at[pl.ds(0, 16)], send.at[1])

    for halo in halos:
        halo.wait()
    rows_x[:, 6:8, :] = halo_x[0]
    rows_x[:, 24:26, :] = halo_x[1]
    grad_x = (
        8.0 * (rows_x[:, 9:25, :] - rows_x[:, 7:23, :])
        - (rows_x[:, 10:26, :] - rows_x[:, 6:22, :])
    ) * scale
    stack = jnp.concatenate([halo_z[0], total, halo_z[1]], axis=0)
    grad_z = (8.0 * (stack[3:7] - stack[1:5]) - (stack[4:8] - stack[0:4])) * scale
    norm = jnp.sqrt(grad_z * grad_z + grad_x * grad_x + grad_y * grad_y)
    reduced = norm / (FERMI_FACTOR * power)
    enhance = 1.0 + KAPPA_PBE - KAPPA_PBE / (1.0 + MU_PBE * reduced * reduced / KAPPA_PBE)
    reduced_ref[...] = reduced
    energy_ref[...] = -SLATER_FACTOR * power * enhance
    store_real.wait()
    store_imag.wait()


def per_device(wavefunctions, potential, occupation):
    any_space = pl.BlockSpec(memory_space=pl.ANY)
    vmem = pl.BlockSpec(memory_space=pltpu.VMEM)
    block = (PLANES, OWN_ROWS, GRID)
    planes = (2, 2, PLANES, GRID, GRID)
    dma = pltpu.SemaphoreType.DMA
    return pl.pallas_call(
        kernel,
        name="taylor_step",
        out_shape=(
            jax.ShapeDtypeStruct(planes, F32),
            jax.ShapeDtypeStruct(block, F32),
            jax.ShapeDtypeStruct(block, F32),
        ),
        in_specs=[pl.BlockSpec(memory_space=pltpu.SMEM), any_space, any_space, any_space],
        out_specs=(any_space, vmem, vmem),
        scratch_shapes=[
            pltpu.VMEM(planes, F32),
            pltpu.VMEM((PLANES, GRID, GRID), F32),
            pltpu.VMEM((2, GRID, GRID), BF16),
            pltpu.VMEM(planes, F32),
            pltpu.VMEM(planes, F32),
            pltpu.VMEM((4, GRID, ROWS, GRID), F32),
            pltpu.VMEM((GRID, ROWS, GRID), F32),
            pltpu.VMEM((2, GRID, ROWS, GRID), F32),
            pltpu.VMEM(planes, F32),
            pltpu.VMEM((PLANES, GRID, GRID), F32),
            pltpu.VMEM((BAND, *block), F32),
            pltpu.VMEM(block, F32),
            pltpu.VMEM((2, 2, OWN_ROWS, GRID), F32),
            pltpu.VMEM((2, PLANES, 2, GRID), F32),
            pltpu.VMEM((2, PLANES, 2, GRID), F32),
            pltpu.VMEM((PLANES, 32, GRID), F32),
            dma((3,)),
            dma((2,)),
            dma,
            dma((2,)),
            dma,
            dma((BAND,)),
            dma((2,)),
            dma,
            dma((4,)),
            dma((10,)),
        ],
        compiler_params=pltpu.CompilerParams(
            collective_id=0, has_side_effects=True, vmem_limit_bytes=40 * 1024 * 1024
        ),
    )(occupation, wavefunctions, potential, kinetic_parts())


def solution(mesh):
    in_specs = (P(None, "band", "fft", None, None), P("fft", None, None), P("band"))
    out_specs = (P(None, "band", "fft", None, None), P("fft", "band", None), P("fft", "band", None))
    return jax.shard_map(
        per_device, mesh=mesh, in_specs=in_specs, out_specs=out_specs, check_vma=False
    )
```

profile of v0, /device:TPU:96, one launch (start us, length us, event | category | flops | bytes accessed | tf_op | source)
XLA Modules:
  0.0 98.3 jit_solution(8347186015115999724)
XLA Ops:
  0.6 0.0 copy-start
  0.6 1.2 %copy-done = f32[2,2,4,128,128]{4,3,2,1,0:T(8,128)S(1)} copy-done((f32[2,2,4,128,128]{4,3,2,1,0:T(8,128)S(1)}, f32[2,2,4,128,128]{4,3,2,1,0:T(8,128)}, u32[]{:S(2)}) %copy-start) | copy-done | bytes 1048600
  1.9 0.0 copy-start.1
  1.9 0.9 copy-done.1
  2.8 0.0 copy-start.2
  2.8 0.8 copy-done.2
  3.6 0.0 copy-start.3
  3.6 0.7 copy-done.3
  4.3 91.8 %taylor_step.1 = (f32[2,2,4,128,128]{4,3,2,1,0:T(8,128)S(1)}, f32[4,16,128]{2,1,0:T(8,128)S(1)}, f32[4,16,128]{2,1,0:T(8,128)S(1)}) custom-call(f32[2]{0:T(128)S(1)} %copy-done.3, f32[2,2,4,128,128]{4,3,2,1,0:T(8,128)S(1)} %copy-done, f32[4,128,128]{2,1,0:T(8,128)S(1)} %copy-done.1, bf16[2,128,128]{2,1,0:T(8,128)(2,1)S(1)} %copy-done.2), custom_call_target="tpu_custom_call" | custom-call | tf_op jit(solution)/shard_map/taylor_step/pallas_call | solution.py:412
  96.1 1.0 copy.10
  97.1 0.6 copy.11
  97.7 0.6 copy.12
Async XLA Ops:
  0.6 1.2 %copy-start = (f32[2,2,4,128,128]{4,3,2,1,0:T(8,128)S(1)}, f32[2,2,4,128,128]{4,3,2,1,0:T(8,128)}, u32[]{:S(2)}) copy-start(f32[2,2,4,128,128]{4,3,2,1,0:T(8,128)} %psi_hbm.1) | copy-start | bytes 3145732
  1.9 0.9 copy-start.1
  2.8 0.8 copy-start.2
  3.6 0.7 copy-start.3
where the time goes:
time: 98.5 us; the launch traced here: 98.3 us
  Pallas kernels  91.8 us (93%)
  local copies, waits for them, and re-layouts  5.86 us (6%)
    pallas_call x1, Pallas kernels, per_device(): pl.pallas_call(kernel, name='taylor_step', out_shape=(jax.ShapeDtypeStruc...  91.8 us
    unnamed x11, local copies, waits for them, and re-layouts  5.86 us

commit v1 on v0

--- a/solution.py
+++ b/solution.py
@@ -41,7 +41,8 @@
     matrix = kinetic_matrix()
     high = matrix.astype(jnp.bfloat16)
     low = (matrix - high.astype(np.float64)).astype(jnp.bfloat16)
-    return np.stack([high, low])
+    beside = np.concatenate([high, high, low], axis=1)
+    return beside, beside.T.copy()
 
 
 def split(values):
@@ -53,16 +54,16 @@
     return jnp.dot(a, b, preferred_element_type=F32)
 
 
-def from_left(table, values):
+def from_left(left, values):
     high, low = split(values)
-    return dot(table[0], high) + dot(table[0], low) + dot(table[1], high)
-
-
-def in_plane(table, values):
+    return dot(left, jnp.concatenate([high, low, high], axis=0))
+
+
+def in_plane(left, right, values):
     high, low = split(values)
-    left = dot(table[0], high) + dot(table[0], low) + dot(table[1], high)
-    right = dot(high, table[0]) + dot(low, table[0]) + dot(high, table[1])
-    return left + right
+    return dot(left, jnp.concatenate([high, low, high], axis=0)) + dot(
+        jnp.concatenate([high, low, high], axis=1), right
+    )
 
 
 def wait_bytes(ref, sem):
@@ -70,16 +71,18 @@
 
 
 def kernel(
-    occ,
+    occ_hbm,
     psi_hbm,
     pot_hbm,
-    table_hbm,
+    left_hbm,
+    right_hbm,
     out_hbm,
-    reduced_ref,
-    energy_ref,
+    summed_ref,
+    occ,
     psi,
     pot,
-    table,
+    left_table,
+    right_table,
     tang,
     local,
     col,
@@ -121,17 +124,14 @@
         return pl.ds(device * PLANES, PLANES)
 
     barrier = pltpu.get_barrier_semaphore()
-    load_psi = pltpu.make_async_copy(psi_hbm, psi, sem_in.at[0])
-    load_pot = pltpu.make_async_copy(pot_hbm, pot, sem_in.at[1])
-    load_table = pltpu.make_async_copy(table_hbm, table, sem_in.at[2])
-    load_psi.start()
-    load_pot.start()
-    load_table.start()
 
     @pl.loop(1, FFT)
     def _(step):
         pl.semaphore_signal(
-            barrier, inc=1, device_id={"fft": fft_peer(step)}, device_id_type=MESH
+            barrier,
+            inc=1,
+            device_id={"fft": lax.rem(me + step, FFT)},
+            device_id_type=MESH,
         )
 
     @pl.loop(1, BAND)
@@ -143,10 +143,44 @@
             device_id_type=MESH,
         )
 
-    load_psi.wait()
-    load_pot.wait()
-    load_table.wait()
+    loads = [
+        pltpu.make_async_copy(source, target, sem_in.at[k])
+        for k, (source, target) in enumerate((
+            (psi_hbm, psi),
+            (pot_hbm, pot),
+            (left_hbm, left_table),
+            (right_hbm, right_table),
+            (occ_hbm, occ),
+        ))
+    ]
+    for load in loads:
+        load.start()
+    for load in loads:
+        load.wait()
     pl.semaphore_wait(barrier, FFT + BAND - 2)
+
+    first_slot = lax.rem(my_band - me + FFT, BAND)
+    for k in range(4):
+        target = 2 * (first_slot + BAND * (k // 2)) + k % 2
+
+        @pl.when(target != me)
+        def _():
+            pltpu.make_async_remote_copy(
+                src_ref=pot.at[:, rows_of(target // 2), :],
+                dst_ref=col_pot.at[planes_of(me)],
+                send_sem=send.at[1],
+                recv_sem=sem_pot.at[0],
+                device_id={"fft": target},
+                device_id_type=MESH,
+            ).start()
+
+        @pl.when(target == me)
+        def _():
+            pltpu.make_async_copy(
+                pot.at[:, rows_of(my_slot), :],
+                col_pot.at[planes_of(me)],
+                sem_pot.at[0],
+            ).start()
 
     @pl.loop(1, FFT)
     def _(step):
@@ -166,37 +200,14 @@
         sem_col,
     ).start()
 
-    first_slot = lax.rem(my_band - me + FFT, BAND)
-    for k in range(4):
-        target = 2 * (first_slot + BAND * (k // 2)) + k % 2
-
-        @pl.when(target != me)
-        def _():
-            pltpu.make_async_remote_copy(
-                src_ref=pot.at[:, rows_of(target // 2), :],
-                dst_ref=col_pot.at[planes_of(me)],
-                send_sem=send.at[1],
-                recv_sem=sem_pot.at[0],
-                device_id={"fft": target},
-                device_id_type=MESH,
-            ).start()
-
-        @pl.when(target == me)
-        def _():
-            pltpu.make_async_copy(
-                pot.at[:, rows_of(my_slot), :],
-                col_pot.at[planes_of(me)],
-                sem_pot.at[0],
-            ).start()
-
-    kin = (table[0], table[1])
+    left, right = left_table[...], right_table[...]
 
     for part_of in range(2):
 
-        @pl.loop(0, 8)
+        @pl.loop(0, 8, unroll=4)
         def _(index):
             band, plane = index // 4, index % 4
-            tang[part_of, band, plane] = in_plane(kin, psi[part_of, band, plane])
+            tang[part_of, band, plane] = in_plane(left, right, psi[part_of, band, plane])
 
         @pl.loop(1, FFT)
         def _(step):
@@ -234,15 +245,15 @@
                 device_id_type=MESH,
             ).start()
 
-    @pl.loop(0, 8)
+    @pl.loop(0, 8, unroll=2)
     def _(index):
         band, plane = index // 4, index % 4
         values = pot[plane]
         real, imag = psi[0, band, plane], psi[1, band, plane]
         first_real = tang[0, band, plane] + values * real
         first_imag = tang[1, band, plane] + values * imag
-        second_real = in_plane(kin, first_real) + values * first_real
-        second_imag = in_plane(kin, first_imag) + values * first_imag
+        second_real = in_plane(left, right, first_real) + values * first_real
+        second_imag = in_plane(left, right, first_imag) + values * first_imag
         local[0, band, plane] = real + TIME_STEP * first_imag - HALF_SQUARE * second_real
         local[1, band, plane] = imag - TIME_STEP * first_real - HALF_SQUARE * second_imag
 
@@ -252,18 +263,24 @@
         sign = 1.0 - 2.0 * part_of
         wait_bytes(col.at[2 + part_of], sem_tang.at[part_of])
 
-        @pl.loop(0, ROWS)
-        def _(row):
-            values = col_pot[:, row, :]
-            mine = col[part_of, :, row, :]
-            other = col[1 - part_of, :, row, :]
-            along = from_left(kin, mine)
+        for pair in range(0, ROWS, 2):
+
+            def rows(ref, *index):
+                return jnp.concatenate(
+                    [ref[(*index, slice(None), pair + k)] for k in range(2)], axis=1
+                )
+
+            values = rows(col_pot)
+            mine = rows(col, part_of)
+            along = from_left(left, mine)
             inner = (
-                (sign * TIME_STEP) * other
-                - (2.0 * HALF_SQUARE) * col[2 + part_of, :, row, :]
+                (sign * TIME_STEP) * rows(col, 1 - part_of)
+                - (2.0 * HALF_SQUARE) * rows(col, 2 + part_of)
                 - HALF_SQUARE * (values * mine + along)
             )
-            back[part_of, :, row, :] = from_left(kin, inner) - HALF_SQUARE * (values * along)
+            moved = from_left(left, inner) - HALF_SQUARE * (values * along)
+            for k in range(2):
+                back[part_of, :, pair + k, :] = moved[:, k * GRID : (k + 1) * GRID]
 
         @pl.loop(1, FFT)
         def _(step):
@@ -367,7 +384,6 @@
         8.0 * (pltpu.roll(total, GRID - 1, 2) - pltpu.roll(total, 1, 2))
         - (pltpu.roll(total, GRID - 2, 2) - pltpu.roll(total, 2, 2))
     ) * scale
-    power = jnp.exp((4.0 / 3.0) * jnp.log(total))
 
     wait_bytes(col.at[pl.ds(0, 2), pl.ds(0, 124)], send.at[0])
     wait_bytes(col.at[pl.ds(0, 2), pl.ds(0, 124)], send.at[2])
@@ -394,35 +410,66 @@
     ) * scale
     stack = jnp.concatenate([halo_z[0], total, halo_z[1]], axis=0)
     grad_z = (8.0 * (stack[3:7] - stack[1:5]) - (stack[4:8] - stack[0:4])) * scale
-    norm = jnp.sqrt(grad_z * grad_z + grad_x * grad_x + grad_y * grad_y)
-    reduced = norm / (FERMI_FACTOR * power)
-    enhance = 1.0 + KAPPA_PBE - KAPPA_PBE / (1.0 + MU_PBE * reduced * reduced / KAPPA_PBE)
-    reduced_ref[...] = reduced
-    energy_ref[...] = -SLATER_FACTOR * power * enhance
+    summed_ref[0] = grad_z * grad_z + grad_x * grad_x + grad_y * grad_y
+    summed_ref[1] = total
     store_real.wait()
     store_imag.wait()
 
 
+def exchange_terms(square, density):
+    power = jnp.exp((4.0 / 3.0) * jnp.log(density))
+    reduced = jnp.sqrt(square) / (FERMI_FACTOR * power)
+    enhance = 1.0 + KAPPA_PBE - KAPPA_PBE / (1.0 + MU_PBE * reduced * reduced / KAPPA_PBE)
+    return reduced, -SLATER_FACTOR * power * enhance
+
+
+def finish(moved_in, summed_in, moved_out, reduced_out, energy_out, buffer, summed, terms, sem_in, sem_out):
+    first = pltpu.make_async_copy(summed_in, summed, sem_in.at[4])
+    first.start()
+    loads = [
+        pltpu.make_async_copy(moved_in.at[k // 2, k % 2], buffer.at[k], sem_in.at[k])
+        for k in range(4)
+    ]
+    stores = [
+        pltpu.make_async_copy(buffer.at[k], moved_out.at[k // 2, k % 2], sem_out.at[k])
+        for k in range(4)
+    ]
+    stores.append(pltpu.make_async_copy(terms.at[0], reduced_out, sem_out.at[4]))
+    stores.append(pltpu.make_async_copy(terms.at[1], energy_out, sem_out.at[5]))
+    for load in loads:
+        load.start()
+    first.wait()
+    terms[0], terms[1] = exchange_terms(summed[0], summed[1])
+    stores[4].start()
+    stores[5].start()
+    for load, store in zip(loads, stores):
+        load.wait()
+        store.start()
+    for store in stores:
+        store.wait()
+
+
 def per_device(wavefunctions, potential, occupation):
-    any_space = pl.BlockSpec(memory_space=pl.ANY)
+    in_hbm = pl.BlockSpec(memory_space=pltpu.HBM)
     vmem = pl.BlockSpec(memory_space=pltpu.VMEM)
     block = (PLANES, OWN_ROWS, GRID)
     planes = (2, 2, PLANES, GRID, GRID)
     dma = pltpu.SemaphoreType.DMA
-    return pl.pallas_call(
+    moved, summed = pl.pallas_call(
         kernel,
         name="taylor_step",
         out_shape=(
             jax.ShapeDtypeStruct(planes, F32),
-            jax.ShapeDtypeStruct(block, F32),
-            jax.ShapeDtypeStruct(block, F32),
+            jax.ShapeDtypeStruct((2, *block), F32),
         ),
-        in_specs=[pl.BlockSpec(memory_space=pltpu.SMEM), any_space, any_space, any_space],
-        out_specs=(any_space, vmem, vmem),
+        in_specs=[in_hbm] * 5,
+        out_specs=(in_hbm, vmem),
         scratch_shapes=[
+            pltpu.SMEM((2,), F32),
             pltpu.VMEM(planes, F32),
             pltpu.VMEM((PLANES, GRID, GRID), F32),
-            pltpu.VMEM((2, GRID, GRID), BF16),
+            pltpu.VMEM((GRID, 3 * GRID), BF16),
+            pltpu.VMEM((3 * GRID, GRID), BF16),
             pltpu.VMEM(planes, F32),
             pltpu.VMEM(planes, F32),
             pltpu.VMEM((4, GRID, ROWS, GRID), F32),
@@ -436,7 +483,7 @@
             pltpu.VMEM((2, PLANES, 2, GRID), F32),
             pltpu.VMEM((2, PLANES, 2, GRID), F32),
             pltpu.VMEM((PLANES, 32, GRID), F32),
-            dma((3,)),
+            dma((5,)),
             dma((2,)),
             dma,
             dma((2,)),
@@ -448,9 +495,28 @@
             dma((10,)),
         ],
         compiler_params=pltpu.CompilerParams(
-            collective_id=0, has_side_effects=True, vmem_limit_bytes=40 * 1024 * 1024
+            collective_id=0, has_side_effects=True, vmem_limit_bytes=67043328
         ),
-    )(occupation, wavefunctions, potential, kinetic_parts())
+    )(occupation, wavefunctions, potential, *kinetic_parts())
+    return pl.pallas_call(
+        finish,
+        name="exchange",
+        out_shape=(
+            jax.ShapeDtypeStruct(planes, F32),
+            jax.ShapeDtypeStruct(block, F32),
+            jax.ShapeDtypeStruct(block, F32),
+        ),
+        in_specs=[in_hbm, in_hbm],
+        out_specs=(in_hbm, in_hbm, in_hbm),
+        scratch_shapes=[
+            pltpu.VMEM((4, PLANES, GRID, GRID), F32),
+            pltpu.VMEM((2, *block), F32),
+            pltpu.VMEM((2, *block), F32),
+            dma((5,)),
+            dma((6,)),
+        ],
+        compiler_params=pltpu.CompilerParams(vmem_limit_bytes=67043328),
+    )(moved, summed)
 
 
 def solution(mesh):

time: 98.5 us -> 93.8 us (0.952)
  the two profiles are of different devices: /device:TPU:96 before, /device:TPU:64 now
where the time goes in v1:
time: 93.8 us; the launch traced here: 93.7 us
  Pallas kernels  93 us (99%)
    pallas_call x1, Pallas kernels, per_device(): pl.pallas_call(kernel, name='taylor_step', out_shape=(jax.ShapeDtypeStruc...  91 us
    pallas_call x1, Pallas kernels, per_device(): pl.pallas_call(finish, name='exchange', out_shape=(jax.ShapeDtypeStruct(p...  2.05 us

profile of v1, /device:TPU:64, one launch (start us, length us, event | category | flops | bytes accessed | tf_op | source)
XLA Modules:
  0.0 93.7 jit_solution(3182546082295139521)
XLA Ops:
  0.6 91.0 %taylor_step.1 = (f32[2,2,4,128,128]{4,3,2,1,0:T(8,128)}, f32[2,4,16,128]{3,2,1,0:T(8,128)}) custom-call(f32[2]{0:T(128)} %occ_hbm.1, f32[2,2,4,128,128]{4,3,2,1,0:T(8,128)} %psi_hbm.1, f32[4,128,128]{2,1,0:T(8,128)} %pot_hbm.1, bf16[128,384]{1,0:T(8,128)(2,1)} %constant.4.clone.left_hbm, bf16[384,128]{1,0:T(8,128)(2,1)} %constant.5.clone.right_hbm), custom_call_target="tpu_custom_call" | custom-call | tf_op jit(solution)/shard_map/taylor_step/pallas_call | solution.py:458
  91.6 2.0 %exchange.1 = (f32[2,2,4,128,128]{4,3,2,1,0:T(8,128)}, f32[4,16,128]{2,1,0:T(8,128)}, f32[4,16,128]{2,1,0:T(8,128)}) custom-call(f32[2,2,4,128,128]{4,3,2,1,0:T(8,128)} %get-tuple-element.5.moved_in, f32[2,4,16,128]{3,2,1,0:T(8,128)} %get-tuple-element.6.summed_in), custom_call_target="tpu_custom_call" | custom-call | tf_op jit(solution)/shard_map/exchange/pallas_call | solution.py:501

commit v2 on v1

--- a/solution.py
+++ b/solution.py
@@ -76,7 +76,7 @@
     pot_hbm,
     left_hbm,
     right_hbm,
-    out_hbm,
+    local,
     summed_ref,
     occ,
     psi,
@@ -84,7 +84,6 @@
     left_table,
     right_table,
     tang,
-    local,
     col,
     col_pot,
     back,
@@ -97,7 +96,6 @@
     halo_x,
     rows_x,
     sem_in,
-    sem_out,
     sem_col,
     sem_tang,
     sem_ret,
@@ -123,26 +121,6 @@
     def planes_of(device):
         return pl.ds(device * PLANES, PLANES)
 
-    barrier = pltpu.get_barrier_semaphore()
-
-    @pl.loop(1, FFT)
-    def _(step):
-        pl.semaphore_signal(
-            barrier,
-            inc=1,
-            device_id={"fft": lax.rem(me + step, FFT)},
-            device_id_type=MESH,
-        )
-
-    @pl.loop(1, BAND)
-    def _(step):
-        pl.semaphore_signal(
-            barrier,
-            inc=1,
-            device_id={"band": lax.rem(my_band + step, BAND)},
-            device_id_type=MESH,
-        )
-
     loads = [
         pltpu.make_async_copy(source, target, sem_in.at[k])
         for k, (source, target) in enumerate((
@@ -155,13 +133,49 @@
     ]
     for load in loads:
         load.start()
+    barrier = pltpu.get_barrier_semaphore()
+
+    def sign_of(step):
+        half = step // 2
+        return FFT + (2 * (step % 2) - 1) * half
+
+    @pl.loop(1, FFT)
+    def _(step):
+        pl.semaphore_signal(
+            barrier,
+            inc=1,
+            device_id={"fft": lax.rem(me + FFT // 2 + sign_of(step), FFT)},
+            device_id_type=MESH,
+        )
+
+    @pl.loop(1, BAND)
+    def _(step):
+        pl.semaphore_signal(
+            barrier,
+            inc=1,
+            device_id={"band": lax.rem(my_band + step, BAND)},
+            device_id_type=MESH,
+        )
+
+    @pl.loop(1, BAND)
+    def _(step):
+        pl.semaphore_signal(
+            barrier,
+            inc=1,
+            device_id={
+                "fft": me + 1 - 2 * (me % 2),
+                "band": lax.rem(my_band + step, BAND),
+            },
+            device_id_type=MESH,
+        )
+
     for load in loads:
         load.wait()
-    pl.semaphore_wait(barrier, FFT + BAND - 2)
+    pl.semaphore_wait(barrier, FFT - 1 + 2 * (BAND - 1))
 
     first_slot = lax.rem(my_band - me + FFT, BAND)
-    for k in range(4):
-        target = 2 * (first_slot + BAND * (k // 2)) + k % 2
+    for k in range(2):
+        target = 2 * (first_slot + BAND * k) + (me // BAND) % 2
 
         @pl.when(target != me)
         def _():
@@ -227,21 +241,22 @@
             sem_tang.at[part_of],
         ).start()
 
-    wait_bytes(col_pot.at[pl.ds(0, 16)], sem_pot.at[0])
-    first_device = lax.rem(my_band - my_slot + FFT, BAND)
-
-    @pl.loop(0, 4)
+    wait_bytes(col_pot.at[pl.ds(0, 8)], sem_pot.at[0])
+    first_device = lax.rem(my_band - my_slot + FFT, BAND) + BAND * (me % 2)
+
+    @pl.loop(0, 2)
     def _(k):
-        held = planes_of(first_device + BAND * k)
-
-        @pl.loop(1, BAND)
+        held = planes_of(first_device + 2 * BAND * k)
+
+        @pl.loop(1, 2 * BAND)
         def _(step):
+            seat = lax.rem(2 * my_band + me % 2 + step, 2 * BAND)
             pltpu.make_async_remote_copy(
                 src_ref=col_pot.at[held],
                 dst_ref=col_pot.at[held],
                 send_sem=send.at[3],
                 recv_sem=sem_pot.at[1],
-                device_id={"band": lax.rem(my_band + step, BAND)},
+                device_id={"fft": 2 * my_slot + seat % 2, "band": seat // 2},
                 device_id_type=MESH,
             ).start()
 
@@ -258,7 +273,7 @@
         local[1, band, plane] = imag - TIME_STEP * first_real - HALF_SQUARE * second_imag
 
     wait_bytes(col.at[pl.ds(0, 2)], sem_col)
-    wait_bytes(col_pot.at[pl.ds(0, 112)], sem_pot.at[1])
+    wait_bytes(col_pot.at[pl.ds(0, 120)], sem_pot.at[1])
     for part_of in range(2):
         sign = 1.0 - 2.0 * part_of
         wait_bytes(col.at[2 + part_of], sem_tang.at[part_of])
@@ -309,9 +324,6 @@
         local[0, 0, plane] = low
         local[0, 1, plane] = high
         part[plane] = occ[0] * (low * low) + occ[1] * (high * high)
-
-    store_real = pltpu.make_async_copy(local.at[0], out_hbm.at[0], sem_out.at[0])
-    store_real.start()
 
     @pl.loop(0, BAND)
     def _(step):
@@ -341,9 +353,6 @@
         def _():
             pltpu.make_async_copy(part.at[:, rows, :], arrived.at[my_band], sem_dens).start()
 
-    store_imag = pltpu.make_async_copy(local.at[1], out_hbm.at[1], sem_out.at[1])
-    store_imag.start()
-
     wait_bytes(arrived, sem_dens)
     total = arrived[0]
     for k in range(1, BAND):
@@ -388,17 +397,19 @@
     wait_bytes(col.at[pl.ds(0, 2), pl.ds(0, 124)], send.at[0])
     wait_bytes(col.at[pl.ds(0, 2), pl.ds(0, 124)], send.at[2])
     wait_bytes(back.at[:, pl.ds(0, 124)], send.at[4])
-    wait_bytes(col_pot.at[pl.ds(0, 112)], send.at[3])
+    wait_bytes(col_pot.at[pl.ds(0, 120)], send.at[3])
     wait_bytes(arrived.at[pl.ds(0, 7)], send.at[5])
-    holds_own = lax.rem(me + my_slot - my_band + FFT, BAND) == 0
+    holds_own = jnp.logical_and(
+        lax.rem(me + my_slot - my_band + FFT, BAND) == 0, me % 2 == (me // BAND) % 2
+    )
 
     @pl.when(holds_own)
     def _():
-        wait_bytes(col_pot.at[pl.ds(0, 12)], send.at[1])
+        wait_bytes(col_pot.at[pl.ds(0, 4)], send.at[1])
 
     @pl.when(jnp.logical_not(holds_own))
     def _():
-        wait_bytes(col_pot.at[pl.ds(0, 16)], send.at[1])
+        wait_bytes(col_pot.at[pl.ds(0, 8)], send.at[1])
 
     for halo in halos:
         halo.wait()
@@ -412,8 +423,6 @@
     grad_z = (8.0 * (stack[3:7] - stack[1:5]) - (stack[4:8] - stack[0:4])) * scale
     summed_ref[0] = grad_z * grad_z + grad_x * grad_x + grad_y * grad_y
     summed_ref[1] = total
-    store_real.wait()
-    store_imag.wait()
 
 
 def exchange_terms(square, density):
@@ -423,27 +432,17 @@
     return reduced, -SLATER_FACTOR * power * enhance
 
 
-def finish(moved_in, summed_in, moved_out, reduced_out, energy_out, buffer, summed, terms, sem_in, sem_out):
-    first = pltpu.make_async_copy(summed_in, summed, sem_in.at[4])
-    first.start()
-    loads = [
-        pltpu.make_async_copy(moved_in.at[k // 2, k % 2], buffer.at[k], sem_in.at[k])
-        for k in range(4)
-    ]
+def finish(moved, summed, moved_out, reduced_out, energy_out, terms, sem_out):
     stores = [
-        pltpu.make_async_copy(buffer.at[k], moved_out.at[k // 2, k % 2], sem_out.at[k])
+        pltpu.make_async_copy(moved.at[k // 2, k % 2], moved_out.at[k // 2, k % 2], sem_out.at[k])
         for k in range(4)
     ]
     stores.append(pltpu.make_async_copy(terms.at[0], reduced_out, sem_out.at[4]))
     stores.append(pltpu.make_async_copy(terms.at[1], energy_out, sem_out.at[5]))
-    for load in loads:
-        load.start()
-    first.wait()
+    for store in stores[:4]:
+        store.start()
     terms[0], terms[1] = exchange_terms(summed[0], summed[1])
-    stores[4].start()
-    stores[5].start()
-    for load, store in zip(loads, stores):
-        load.wait()
+    for store in stores[4:]:
         store.start()
     for store in stores:
         store.wait()
@@ -459,18 +458,17 @@
         kernel,
         name="taylor_step",
         out_shape=(
-            jax.ShapeDtypeStruct(planes, F32),
-            jax.ShapeDtypeStruct((2, *block), F32),
+            pltpu.VMEM(planes, F32),
+            pltpu.VMEM((2, *block), F32),
         ),
         in_specs=[in_hbm] * 5,
-        out_specs=(in_hbm, vmem),
+        out_specs=(vmem, vmem),
         scratch_shapes=[
             pltpu.SMEM((2,), F32),
             pltpu.VMEM(planes, F32),
             pltpu.VMEM((PLANES, GRID, GRID), F32),
             pltpu.VMEM((GRID, 3 * GRID), BF16),
             pltpu.VMEM((3 * GRID, GRID), BF16),
-            pltpu.VMEM(planes, F32),
             pltpu.VMEM(planes, F32),
             pltpu.VMEM((4, GRID, ROWS, GRID), F32),
             pltpu.VMEM((GRID, ROWS, GRID), F32),
@@ -484,7 +482,6 @@
             pltpu.VMEM((2, PLANES, 2, GRID), F32),
             pltpu.VMEM((PLANES, 32, GRID), F32),
             dma((5,)),
-            dma((2,)),
             dma,
             dma((2,)),
             dma,
@@ -495,7 +492,7 @@
             dma((10,)),
         ],
         compiler_params=pltpu.CompilerParams(
-            collective_id=0, has_side_effects=True, vmem_limit_bytes=67043328
+            collective_id=0, has_side_effects=True, vmem_limit_bytes=62000000
         ),
     )(occupation, wavefunctions, potential, *kinetic_parts())
     return pl.pallas_call(
@@ -506,16 +503,13 @@
             jax.ShapeDtypeStruct(block, F32),
             jax.ShapeDtypeStruct(block, F32),
         ),
-        in_specs=[in_hbm, in_hbm],
+        in_specs=[vmem, vmem],
         out_specs=(in_hbm, in_hbm, in_hbm),
         scratch_shapes=[
-            pltpu.VMEM((4, PLANES, GRID, GRID), F32),
             pltpu.VMEM((2, *block), F32),
-            pltpu.VMEM((2, *block), F32),
-            dma((5,)),
             dma((6,)),
         ],
-        compiler_params=pltpu.CompilerParams(vmem_limit_bytes=67043328),
+        compiler_params=pltpu.CompilerParams(vmem_limit_bytes=16000000),
     )(moved, summed)
 
 

time: 93.8 us -> 91.5 us (0.975)
  Pallas kernels: 93 us -> 90.3 us
    pallas_call x1, Pallas kernels: 91 us -> 89.2 us  [per_device(): pl.pallas_call(kernel, name='taylor_step', out_shape=(pltpu.VMEM(planes,...]
    pallas_call x1, Pallas kernels: 2.05 us -> 1.03 us  [per_device(): pl.pallas_call(finish, name='exchange', out_shape=(jax.ShapeDtypeStruct(p...]
where the time goes in v2:
time: 91.5 us; the launch traced here: 90.9 us
  Pallas kernels  90.3 us (99%)
    pallas_call x1, Pallas kernels, per_device(): pl.pallas_call(kernel, name='taylor_step', out_shape=(pltpu.VMEM(planes,...  89.2 us

profile of v2, /device:TPU:64, one launch (start us, length us, event | category | flops | bytes accessed | tf_op | source)
XLA Modules:
  0.0 90.9 jit_solution(11398009875751269375)
XLA Ops:
  0.6 89.2 %taylor_step.1 = (f32[2,2,4,128,128]{4,3,2,1,0:T(8,128)S(1)}, f32[2,4,16,128]{3,2,1,0:T(8,128)S(1)}) custom-call(f32[2]{0:T(128)} %occ_hbm.1, f32[2,2,4,128,128]{4,3,2,1,0:T(8,128)} %psi_hbm.1, f32[4,128,128]{2,1,0:T(8,128)} %pot_hbm.1, bf16[128,384]{1,0:T(8,128)(2,1)} %constant.4.clone.left_hbm, bf16[384,128]{1,0:T(8,128)(2,1)} %constant.5.clone.right_hbm), custom_call_target="tpu_custom_call" | custom-call | tf_op jit(solution)/shard_map/taylor_step/pallas_call | solution.py:457
  89.9 1.0 %exchange.1 = (f32[2,2,4,128,128]{4,3,2,1,0:T(8,128)}, f32[4,16,128]{2,1,0:T(8,128)}, f32[4,16,128]{2,1,0:T(8,128)}) custom-call(f32[2,2,4,128,128]{4,3,2,1,0:T(8,128)S(1)} %get-tuple-element.5.moved, f32[2,4,16,128]{3,2,1,0:T(8,128)S(1)} %get-tuple-element.6.summed), custom_call_target="tpu_custom_call" | custom-call | tf_op jit(solution)/shard_map/exchange/pallas_call | solution.py:498

commit v3 on v2

--- a/solution.py
+++ b/solution.py
@@ -104,6 +104,8 @@
     sem_dens,
     sem_halo,
     send,
+    sem_group_in,
+    sem_groups_in,
 ):
     me = lax.axis_index("fft")
     my_band = lax.axis_index("band")
@@ -148,30 +150,25 @@
             device_id_type=MESH,
         )
 
-    @pl.loop(1, BAND)
-    def _(step):
-        pl.semaphore_signal(
-            barrier,
-            inc=1,
-            device_id={"band": lax.rem(my_band + step, BAND)},
-            device_id_type=MESH,
-        )
-
-    @pl.loop(1, BAND)
-    def _(step):
-        pl.semaphore_signal(
-            barrier,
-            inc=1,
-            device_id={
-                "fft": me + 1 - 2 * (me % 2),
-                "band": lax.rem(my_band + step, BAND),
-            },
-            device_id_type=MESH,
-        )
+    stands = jnp.logical_and(me >= 1, me < BAND)
+    ahead = {"band": lax.rem(my_band + me, BAND)}
+    behind = {"band": lax.rem(my_band - me + FFT, BAND)}
+
+    @pl.when(stands)
+    def _():
+        pl.semaphore_signal(barrier, inc=1, device_id=ahead, device_id_type=MESH)
 
     for load in loads:
         load.wait()
-    pl.semaphore_wait(barrier, FFT - 1 + 2 * (BAND - 1))
+    @pl.when(jnp.logical_not(stands))
+    def _():
+        pl.semaphore_wait(barrier, FFT - 1)
+
+    @pl.when(stands)
+    def _():
+        pl.semaphore_wait(barrier, FFT)
+        pl.semaphore_signal(sem_group_in, inc=1, device_id=behind, device_id_type=MESH)
+
 
     first_slot = lax.rem(my_band - me + FFT, BAND)
     for k in range(2):
@@ -240,6 +237,22 @@
             col.at[2 + part_of, planes_of(me)],
             sem_tang.at[part_of],
         ).start()
+
+    @pl.when(stands)
+    def _():
+        pl.semaphore_wait(sem_group_in, 1)
+        pl.semaphore_signal(sem_groups_in, inc=1)
+
+        @pl.loop(1, FFT)
+        def _(step):
+            pl.semaphore_signal(
+                sem_groups_in,
+                inc=1,
+                device_id={"fft": lax.rem(me + step, FFT)},
+                device_id_type=MESH,
+            )
+
+    pl.semaphore_wait(sem_groups_in, BAND - 1)
 
     wait_bytes(col_pot.at[pl.ds(0, 8)], sem_pot.at[0])
     first_device = lax.rem(my_band - my_slot + FFT, BAND) + BAND * (me % 2)
@@ -490,6 +503,8 @@
             dma,
             dma((4,)),
             dma((10,)),
+            pltpu.SemaphoreType.REGULAR,
+            pltpu.SemaphoreType.REGULAR,
         ],
         compiler_params=pltpu.CompilerParams(
             collective_id=0, has_side_effects=True, vmem_limit_bytes=62000000

time: 91.5 us -> 90 us (0.984)
  Pallas kernels: 90.3 us -> 88.6 us
    pallas_call x1, Pallas kernels: 89.2 us -> 87.5 us  [per_device(): pl.pallas_call(kernel, name='taylor_step', out_shape=(pltpu.VMEM(planes,...]
where the time goes in v3:
time: 90 us; the launch traced here: 89.2 us
  Pallas kernels  88.6 us (98%)
    pallas_call x1, Pallas kernels, per_device(): pl.pallas_call(kernel, name='taylor_step', out_shape=(pltpu.VMEM(planes,...  87.5 us

profile of v3, /device:TPU:64, one launch (start us, length us, event | category | flops | bytes accessed | tf_op | source)
XLA Modules:
  0.0 89.2 jit_solution(8492377663469456151)
XLA Ops:
  0.6 87.5 %taylor_step.1 = (f32[2,2,4,128,128]{4,3,2,1,0:T(8,128)S(1)}, f32[2,4,16,128]{3,2,1,0:T(8,128)S(1)}) custom-call(f32[2]{0:T(128)} %occ_hbm.1, f32[2,2,4,128,128]{4,3,2,1,0:T(8,128)} %psi_hbm.1, f32[4,128,128]{2,1,0:T(8,128)} %pot_hbm.1, bf16[128,384]{1,0:T(8,128)(2,1)} %constant.4.clone.left_hbm, bf16[384,128]{1,0:T(8,128)(2,1)} %constant.5.clone.right_hbm), custom_call_target="tpu_custom_call" | custom-call | tf_op jit(solution)/shard_map/taylor_step/pallas_call | solution.py:470
  88.2 1.0 %exchange.1 = (f32[2,2,4,128,128]{4,3,2,1,0:T(8,128)}, f32[4,16,128]{2,1,0:T(8,128)}, f32[4,16,128]{2,1,0:T(8,128)}) custom-call(f32[2,2,4,128,128]{4,3,2,1,0:T(8,128)S(1)} %get-tuple-element.5.moved, f32[2,4,16,128]{3,2,1,0:T(8,128)S(1)} %get-tuple-element.6.summed), custom_call_target="tpu_custom_call" | custom-call | tf_op jit(solution)/shard_map/exchange/pallas_call | solution.py:513

commit v4 on v3

--- a/solution.py
+++ b/solution.py
@@ -117,6 +117,14 @@
         sign = 2 * (step % 2) - 1
         return lax.rem(me + sign * k + FFT, FFT)
 
+    def ring_peer(step):
+        past = step - 4
+        away = jnp.where(step < 4, 0, past // 8 + 1)
+        sign = 1 - 2 * (past % 2)
+        turn = jnp.where(step < 4, step, jnp.where(step < 28, (past % 8) // 2, past % 4))
+        chip = lax.rem(my_chip + sign * away + BAND, BAND)
+        return chip * 4 + lax.rem(me + turn, 4)
+
     def rows_of(slot):
         return pl.ds(pl.multiple_of(slot * ROWS, ROWS), ROWS)
 
@@ -195,7 +203,7 @@
 
     @pl.loop(1, FFT)
     def _(step):
-        peer = fft_peer(step)
+        peer = ring_peer(step)
         pltpu.make_async_remote_copy(
             src_ref=psi.at[:, peer % 2, :, rows_of(peer // 2), :],
             dst_ref=col.at[pl.ds(0, 2), planes_of(me)],
@@ -222,7 +230,7 @@
 
         @pl.loop(1, FFT)
         def _(step):
-            peer = fft_peer(step)
+            peer = ring_peer(step)
             pltpu.make_async_remote_copy(
                 src_ref=tang.at[part_of, peer % 2, :, rows_of(peer // 2), :],
                 dst_ref=col.at[2 + part_of, planes_of(me)],
@@ -312,7 +320,7 @@
 
         @pl.loop(1, FFT)
         def _(step):
-            peer = fft_peer(step)
+            peer = ring_peer(step)
             pltpu.make_async_remote_copy(
                 src_ref=back.at[part_of, planes_of(peer)],
                 dst_ref=ret.at[part_of, me % 2, :, rows_of(my_slot), :],

time: 90 us -> 89.6 us (level)
  no operation moved by 1% of the time
where the time goes in v4:
time: 89.6 us; the launch traced here: 89.1 us
  Pallas kernels  88.5 us (99%)
    pallas_call x1, Pallas kernels, per_device(): pl.pallas_call(kernel, name='taylor_step', out_shape=(pltpu.VMEM(planes,...  87.4 us

profile of v4, /device:TPU:64, one launch (start us, length us, event | category | flops | bytes accessed | tf_op | source)
XLA Modules:
  0.0 89.1 jit_solution(2468857443331849758)
XLA Ops:
  0.6 87.4 %taylor_step.1 = (f32[2,2,4,128,128]{4,3,2,1,0:T(8,128)S(1)}, f32[2,4,16,128]{3,2,1,0:T(8,128)S(1)}) custom-call(f32[2]{0:T(128)} %occ_hbm.1, f32[2,2,4,128,128]{4,3,2,1,0:T(8,128)} %psi_hbm.1, f32[4,128,128]{2,1,0:T(8,128)} %pot_hbm.1, bf16[128,384]{1,0:T(8,128)(2,1)} %constant.4.clone.left_hbm, bf16[384,128]{1,0:T(8,128)(2,1)} %constant.5.clone.right_hbm), custom_call_target="tpu_custom_call" | custom-call | tf_op jit(solution)/shard_map/taylor_step/pallas_call | solution.py:478
  88.1 1.0 %exchange.1 = (f32[2,2,4,128,128]{4,3,2,1,0:T(8,128)}, f32[4,16,128]{2,1,0:T(8,128)}, f32[4,16,128]{2,1,0:T(8,128)}) custom-call(f32[2,2,4,128,128]{4,3,2,1,0:T(8,128)S(1)} %get-tuple-element.5.moved, f32[2,4,16,128]{3,2,1,0:T(8,128)S(1)} %get-tuple-element.6.summed), custom_call_target="tpu_custom_call" | custom-call | tf_op jit(solution)/shard_map/exchange/pallas_call | solution.py:521

commit v5 on v4

--- a/solution.py
+++ b/solution.py
@@ -415,23 +415,6 @@
         - (pltpu.roll(total, GRID - 2, 2) - pltpu.roll(total, 2, 2))
     ) * scale
 
-    wait_bytes(col.at[pl.ds(0, 2), pl.ds(0, 124)], send.at[0])
-    wait_bytes(col.at[pl.ds(0, 2), pl.ds(0, 124)], send.at[2])
-    wait_bytes(back.at[:, pl.ds(0, 124)], send.at[4])
-    wait_bytes(col_pot.at[pl.ds(0, 120)], send.at[3])
-    wait_bytes(arrived.at[pl.ds(0, 7)], send.at[5])
-    holds_own = jnp.logical_and(
-        lax.rem(me + my_slot - my_band + FFT, BAND) == 0, me % 2 == (me // BAND) % 2
-    )
-
-    @pl.when(holds_own)
-    def _():
-        wait_bytes(col_pot.at[pl.ds(0, 4)], send.at[1])
-
-    @pl.when(jnp.logical_not(holds_own))
-    def _():
-        wait_bytes(col_pot.at[pl.ds(0, 8)], send.at[1])
-
     for halo in halos:
         halo.wait()
     rows_x[:, 6:8, :] = halo_x[0]
@@ -444,6 +427,23 @@
     grad_z = (8.0 * (stack[3:7] - stack[1:5]) - (stack[4:8] - stack[0:4])) * scale
     summed_ref[0] = grad_z * grad_z + grad_x * grad_x + grad_y * grad_y
     summed_ref[1] = total
+
+    wait_bytes(col.at[pl.ds(0, 2), pl.ds(0, 124)], send.at[0])
+    wait_bytes(col.at[pl.ds(0, 2), pl.ds(0, 124)], send.at[2])
+    wait_bytes(back.at[:, pl.ds(0, 124)], send.at[4])
+    wait_bytes(col_pot.at[pl.ds(0, 120)], send.at[3])
+    wait_bytes(arrived.at[pl.ds(0, 7)], send.at[5])
+    holds_own = jnp.logical_and(
+        lax.rem(me + my_slot - my_band + FFT, BAND) == 0, me % 2 == (me // BAND) % 2
+    )
+
+    @pl.when(holds_own)
+    def _():
+        wait_bytes(col_pot.at[pl.ds(0, 4)], send.at[1])
+
+    @pl.when(jnp.logical_not(holds_own))
+    def _():
+        wait_bytes(col_pot.at[pl.ds(0, 8)], send.at[1])
 
 
 def exchange_terms(square, density):

time: 89.6 us -> 89.6 us (level)
  no operation moved by 1% of the time
where the time goes in v5:
time: 89.6 us; the launch traced here: 89.1 us
  Pallas kernels  88.5 us (99%)
    pallas_call x1, Pallas kernels, per_device(): pl.pallas_call(kernel, name='taylor_step', out_shape=(pltpu.VMEM(planes,...  87.4 us

profile of v5, /device:TPU:64, one launch (start us, length us, event | category | flops | bytes accessed | tf_op | source)
XLA Modules:
  0.0 89.1 jit_solution(4064267734570253569)
XLA Ops:
  0.6 87.4 %taylor_step.1 = (f32[2,2,4,128,128]{4,3,2,1,0:T(8,128)S(1)}, f32[2,4,16,128]{3,2,1,0:T(8,128)S(1)}) custom-call(f32[2]{0:T(128)} %occ_hbm.1, f32[2,2,4,128,128]{4,3,2,1,0:T(8,128)} %psi_hbm.1, f32[4,128,128]{2,1,0:T(8,128)} %pot_hbm.1, bf16[128,384]{1,0:T(8,128)(2,1)} %constant.4.clone.left_hbm, bf16[384,128]{1,0:T(8,128)(2,1)} %constant.5.clone.right_hbm), custom_call_target="tpu_custom_call" | custom-call | tf_op jit(solution)/shard_map/taylor_step/pallas_call | solution.py:478
  88.1 1.0 %exchange.1 = (f32[2,2,4,128,128]{4,3,2,1,0:T(8,128)}, f32[4,16,128]{2,1,0:T(8,128)}, f32[4,16,128]{2,1,0:T(8,128)}) custom-call(f32[2,2,4,128,128]{4,3,2,1,0:T(8,128)S(1)} %get-tuple-element.5.moved, f32[2,4,16,128]{3,2,1,0:T(8,128)S(1)} %get-tuple-element.6.summed), custom_call_target="tpu_custom_call" | custom-call | tf_op jit(solution)/shard_map/exchange/pallas_call | solution.py:521
